TPU v7x, 32 devices: a whole 2x2x4 slice. The times are simulated.
32 devices in a mesh: section: 2 (over x), fsdp: 16 (over z, y, core).
Axes of the slice: x: 2, y: 2, z: 4, core: 2. Of those that a mesh axis runs over, the one named last changes fastest.
Arguments:
- tokens: bfloat16 [6, 512, 4096], P(None, 'fsdp'), may hold values from -6 to 6
- cotangent: bfloat16 [6, 512, 4096], P(None, 'fsdp'), may hold values from -6 to 6
- order: int32 [6], replicated, may hold values from 0 to 5, each once
- w_value: bfloat16 [2, 4096, 512], P('section', 'fsdp'), may hold values from -0.09375 to 0.09375
- w_out: bfloat16 [2, 512, 4096], P('section', None, 'fsdp'), may hold values from -0.25 to 0.25
- adapter_down: bfloat16 [2, 4096, 128], P('section', 'fsdp'), may hold values from -0.09375 to 0.09375
- adapter_up: bfloat16 [2, 128, 512], P('section', None, 'fsdp'), may hold values from -0.5 to 0.5
Outputs:
- input_grads: bfloat16 [2, 6, 512, 4096], P('section', None, 'fsdp')
- grad_down: float32 [2, 4096, 128], P('section', 'fsdp')
- grad_up: float32 [2, 128, 512], P('section', None, 'fsdp')
Inputs may be any that keep to these rules, and one draw needn't show every extreme that they name: order names each microbatch 0 .. 5 exactly once.
All inputs are finite; a program needn't handle non-finite values.
Results may differ from a plain program's by a relative error of at most 0.02.
Values may be sent and summed in bfloat16 or wider, within the bound.
A program may use at most 128 MiB of HBM per device.

v0:
```python
import functools

import jax
import jax.numpy as jnp
from jax import lax
from jax.experimental import pallas as pl
from jax.experimental.pallas import tpu as pltpu
from jax.sharding import PartitionSpec as P

epsilon = 1e-05
MESH = pl.DeviceIdType.MESH
X, Y, Z = 0, 1, 2


def plan_of(shapes):
    half0, half1 = shapes[0][0] // 2, shapes[1][0] // 2
    return (
        (0, 0, half0, (Y, Z, X)),
        (0, half0, half0, (X, Z, Y)),
        (1, 0, half1, (Z, Y, X)),
        (1, half1, half1, (Z, X, Y)),
        (2, 0, shapes[2][0], (Z, Y, X)),
    )


def spread_kernel(lines, plan, a_ref, b_ref, c_ref, a_out, b_out, c_out, own_sem, recv_sem, send_sem):
    sources, outs = (a_ref, b_ref, c_ref), (a_out, b_out, c_out)
    fsdp = lines * 4
    s, f = lax.axis_index("section"), lax.axis_index("fsdp")
    core, y, z = f % 2, (f // 2) % 2, f // 4

    def place(s_, z_, y_, c_):
        return {"section": s_, "fsdp": (z_ * 2 + y_) * 2 + c_}

    partner = place(s, z, y, 1 - core)
    across = place(1 - s, z, y, core)
    beside = place(s, z, 1 - y, core)
    above = place(s, z + 1, y, core)
    below = place(s, z - 1, y, core)

    barrier = pltpu.get_barrier_semaphore()
    for target in (partner, across, beside):
        pl.semaphore_signal(barrier, inc=1, device_id=target, device_id_type=MESH)

    @pl.when(z + 1 < lines)
    def _():
        pl.semaphore_signal(barrier, inc=1, device_id=above, device_id_type=MESH)

    @pl.when(z > 0)
    def _():
        pl.semaphore_signal(barrier, inc=1, device_id=below, device_id_type=MESH)

    ends = (z + 1 < lines).astype(jnp.int32) + (z > 0).astype(jnp.int32)
    pl.semaphore_wait(barrier, 3 + ends)

    def when(test, action):
        if test is True:
            action()
        else:
            pl.when(test)(action)

    def both(left, right):
        return right if left is True else left if right is True else left & right

    def slot_of(dx, dy, dz, c_):
        return ((s + dx) % 2) * fsdp + ((z + dz) * 2 + (y + dy) % 2) * 2 + c_

    def piece(index, slot):
        array, first, rows, _ = plan[index]
        return outs[array].at[slot, pl.ds(first, rows)]

    def sends(index, dx, dy, dz, step):
        array, first, rows, order = plan[index]
        slot = slot_of(dx, dy, dz, core)
        own = dx == 0 and dy == 0 and dz == 0
        source = sources[array].at[pl.ds(first, rows)] if own else piece(index, slot)
        gone = {X: dx != 0, Y: dy != 0, Z: dz != 0}
        result = []

        def add(way, test, target):
            copy = pltpu.make_async_remote_copy(
                src_ref=source,
                dst_ref=piece(index, slot),
                send_sem=send_sem.at[step * 5 + way],
                recv_sem=recv_sem.at[slot * len(plan) + index],
                device_id=target,
                device_id_type=MESH,
            )
            result.append((test, copy))

        for rank, dim in enumerate(order):
            if any(gone[later] for later in order[rank + 1:]):
                continue
            if dim == Z:
                if dz <= 0:
                    add(0, z + 1 < lines, above)
                if dz >= 0:
                    add(1, z > 0, below)
            elif not gone[dim]:
                add(2 + dim, True, across if dim == X else beside)
        add(4, True, partner)
        return result

    events = []
    for dx in (0, 1):
        for dy in (0, 1):
            for dz in range(1 - lines, lines):
                for index in range(len(plan)):
                    events.append((dx + dy + abs(dz), index, dx, dy, dz))
    events.sort(key=lambda event: (event[0], abs(event[4]), event[1]))
    steps = {}

    def step_of(index, dx, dy, dz):
        return steps.setdefault((index, dx, dy, dz % lines), len(steps))

    def inside(dz):
        return True if dz == 0 else (z + dz < lines) if dz > 0 else (z + dz >= 0)

    copies = []
    for array in range(3):
        copy = pltpu.make_async_copy(sources[array], outs[array].at[slot_of(0, 0, 0, core)], own_sem.at[array])
        copy.start()
        copies.append(copy)

    def arrival(index, slot):
        ref = piece(index, slot)
        sem = recv_sem.at[slot * len(plan) + index]
        pltpu.make_async_copy(ref, ref, sem).wait()

    def run(event):
        distance, index, dx, dy, dz = event
        step = step_of(index, dx, dy, dz)

        def action():
            if distance:
                arrival(index, slot_of(dx, dy, dz, core))
            for test, copy in sends(index, dx, dy, dz, step):
                when(test, copy.start)

        when(inside(dz), action)

    for event in events:
        run(event)
    for _, index, dx, dy, dz in events:
        when(inside(dz), functools.partial(arrival, index, slot_of(dx, dy, dz, 1 - core)))
    for copy in copies:
        copy.wait()
    for _, index, dx, dy, dz in events:
        for test, copy in sends(index, dx, dy, dz, step_of(index, dx, dy, dz)):
            when(both(inside(dz), test), copy.wait_send)


def spread(joined, proj, up):
    fsdp = lax.axis_size("fsdp")
    devices = fsdp * lax.axis_size("section")
    blocks = (joined, proj, up)
    plan = plan_of([block.shape for block in blocks])
    pieces = len(plan)
    return pl.pallas_call(
        functools.partial(spread_kernel, fsdp // 4, plan),
        out_shape=[jax.ShapeDtypeStruct((devices,) + b.shape, b.dtype) for b in blocks],
        in_specs=[pl.BlockSpec(memory_space=pltpu.VMEM)] * 3,
        out_specs=[pl.BlockSpec(memory_space=pl.ANY)] * 3,
        scratch_shapes=[
            pltpu.SemaphoreType.DMA((3,)),
            pltpu.SemaphoreType.DMA((devices * pieces,)),
            pltpu.SemaphoreType.DMA((fsdp * pieces * 5,)),
        ],
        compiler_params=pltpu.CompilerParams(collective_id=0, has_side_effects=True),
    )(*blocks)


def settle_kernel(parts_ref, down_ref, up_ref, near, mine, far, near_send, near_recv, far_send, far_recv):
    chips = parts_ref.shape[0]
    f = lax.axis_index("fsdp")
    core, chip = f % 2, f // 2
    barrier = pltpu.get_barrier_semaphore()
    pl.semaphore_signal(barrier, inc=1, device_id={"fsdp": chip * 2 + 1 - core}, device_id_type=MESH)
    for step in range(1, chips):
        other = (chip + step) % chips
        pl.semaphore_signal(barrier, inc=1, device_id={"fsdp": other * 2 + core}, device_id_type=MESH)
    pl.semaphore_wait(barrier, chips)

    handed, passed = [], []
    for step in range(chips):
        other = (chip + 1 + step) % chips
        copy = pltpu.make_async_remote_copy(
            src_ref=parts_ref.at[other, 1 - core],
            dst_ref=near.at[step],
            send_sem=near_send.at[step],
            recv_sem=near_recv.at[step],
            device_id={"fsdp": chip * 2 + 1 - core},
            device_id_type=MESH,
        )
        copy.start()
        handed.append(copy)
    for step in range(chips - 1):
        other = (chip + 1 + step) % chips
        handed[step].wait_recv()
        mine[step] = (
            parts_ref[other, core].astype(jnp.float32) + near[step].astype(jnp.float32)
        ).astype(mine.dtype)
        copy = pltpu.make_async_remote_copy(
            src_ref=mine.at[step],
            dst_ref=far.at[step],
            send_sem=far_send.at[step],
            recv_sem=far_recv.at[step],
            device_id={"fsdp": other * 2 + core},
            device_id_type=MESH,
        )
        passed.append(copy)
        if step:
            passed[step - 1].start()
    handed[-1].wait_recv()
    total = parts_ref[chip, core].astype(jnp.float32) + near[chips - 1].astype(jnp.float32)
    passed[-1].start()
    for step in range(chips - 1):
        passed[step].wait_recv()
        total = total + far[step].astype(jnp.float32)
    split = down_ref.shape[0]
    down_ref[...] = total[:split]
    up_ref[...] = total[split:]
    for copy in handed + passed:
        copy.wait_send()


def settle(parts, split):
    chips, _, rows, rank = parts.shape
    buffer = pltpu.VMEM((chips, rows, rank), parts.dtype)
    return pl.pallas_call(
        settle_kernel,
        out_shape=[
            jax.ShapeDtypeStruct((split, rank), jnp.float32),
            jax.ShapeDtypeStruct((rows - split, rank), jnp.float32),
        ],
        in_specs=[pl.BlockSpec(memory_space=pltpu.VMEM)],
        out_specs=[pl.BlockSpec(memory_space=pltpu.VMEM)] * 2,
        scratch_shapes=[buffer, buffer, buffer] + [pltpu.SemaphoreType.DMA((chips,))] * 4,
        compiler_params=pltpu.CompilerParams(collective_id=1, has_side_effects=True),
    )(parts)


def widen_dot(left, right, dims=((1,), (0,))):
    return lax.dot_general(left, right, (dims, ((), ())), preferred_element_type=jnp.float32)


def layers_kernel(
    sections, width, order_ref, tok_ref, cot_ref, wa_any, wo_any, up_any, out_ref, parts_ref,
    wa, wo, up, states, normed, low, cats, wide, flow, acc, sems,
):
    rows, features = tok_ref.shape
    micro = out_ref.shape[0]
    step = width
    steps = features // step
    position = lax.axis_index("section")
    bf16, f32 = jnp.bfloat16, jnp.float32
    pending = {}
    for layer in range(sections):
        for kind, (source, target) in enumerate(((wa_any, wa), (up_any, up), (wo_any, wo))):
            copy = pltpu.make_async_copy(
                source.at[layer], target.at[layer], sems.at[layer * 3 + kind]
            )
            copy.start()
            pending[layer, kind] = copy

    def ready(layer, kind):
        if (layer, kind) in pending:
            pending.pop((layer, kind)).wait()

    def span(index):
        return pl.ds(pl.multiple_of(index * step, step), step)

    def loop(action, start):
        return lax.fori_loop(0, steps, action, start)

    zero = jnp.zeros((rows, 1), f32)

    def state(layer):
        return tok_ref if layer == 0 else states.at[layer - 1]

    def squares(index, total):
        piece = tok_ref[:, span(index)].astype(f32)
        return total + jnp.sum(piece * piece, axis=1, keepdims=True)

    total = loop(squares, zero)
    inverses = []
    for layer in range(sections):
        last = layer == sections - 1
        inverse = lax.rsqrt(total / features + epsilon)
        inverses.append(inverse)
        ready(layer, 0)
        start = width if last else 0
        acc[...] = jnp.zeros_like(acc)

        def project(index, carry, layer=layer, inverse=inverse, start=start):
            piece = (state(layer)[:, span(index)].astype(f32) * inverse).astype(bf16)
            normed[layer, :, span(index)] = piece
            acc[:, start:] += widen_dot(piece, wa[layer, span(index), start:])
            return carry

        loop(project, 0)
        low[layer] = acc[:, width:].astype(bf16)
        ready(layer, 1)
        ready(layer, 2)
        if not last:
            values = (acc[:, :width] + widen_dot(low[layer], up[layer], ((1,), (1,)))).astype(bf16)
            cats[layer, :, :width] = values

            def widen(index, carry, layer=layer):
                added = widen_dot(cats[layer, :, :width], wo[layer, span(index), :], ((1,), (1,)))
                piece = (state(layer)[:, span(index)].astype(f32) + added).astype(bf16)
                states[layer, :, span(index)] = piece
                back = piece.astype(f32)
                return carry + jnp.sum(back * back, axis=1, keepdims=True)

            total = loop(widen, zero)

    def backward(layer):
        upstream = cot_ref if layer == sections - 1 else flow.at[layer + 1]
        inverse = inverses[layer]
        acc[:, :width] = jnp.zeros((rows, width), f32)

        def narrow(index, carry):
            acc[:, :width] += widen_dot(upstream[:, span(index)], wo[layer, span(index), :])
            return carry

        loop(narrow, 0)
        d_values = acc[:, :width].astype(bf16)
        cats[layer, :, :width] = d_values
        cats[layer, :, width:] = widen_dot(d_values, up[layer]).astype(bf16)

        def open_up(index, carry):
            piece = widen_dot(cats[layer], wa[layer, span(index), :], ((1,), (1,)))
            wide[:, span(index)] = piece
            inputs = state(layer)[:, span(index)].astype(f32)
            return carry + jnp.sum(piece * inputs, axis=1, keepdims=True)

        mean = loop(open_up, zero) / features

        def finish(index, carry):
            inputs = state(layer)[:, span(index)].astype(f32)
            piece = upstream[:, span(index)].astype(f32) + inverse * (
                wide[:, span(index)] - inputs * inverse * inverse * mean
            )
            flow[layer, :, span(index)] = piece.astype(bf16)
            return carry

        loop(finish, 0)

    for layer in reversed(range(sections)):
        if layer == sections - 1:
            backward(layer)
        else:
            pl.when(position <= layer)(functools.partial(backward, layer))

    blocks = parts_ref.shape[0]
    share, share_up = features // blocks, width // blocks

    def contract(index, carry):
        columns = pl.ds(pl.multiple_of(index * share, share), share)
        parts_ref[index, :share, :] = widen_dot(
            normed[position, :, columns], cats[position, :, width:], ((0,), (0,))
        ).astype(bf16)
        return carry

    lax.fori_loop(0, blocks, contract, 0)
    both = widen_dot(cats[position, :, :width], low[position], ((0,), (0,))).astype(bf16)
    for index in range(blocks):
        parts_ref[index, share:, :] = both[index * share_up:(index + 1) * share_up]
    local = rows // micro
    for slot in range(micro):
        out_ref[slot] = flow[position, pl.ds(pl.multiple_of(order_ref[slot] * local, local), local), :]


def run_layers(tokens, cotangent, order, joined, proj, up):
    micro, local, features = tokens.shape
    sections, _, width = proj.shape
    rank = up.shape[2]
    rows = micro * local
    shares = lax.axis_size("fsdp")
    block = (features + width) // shares
    bf16, f32 = jnp.bfloat16, jnp.float32
    inside, outside = pl.BlockSpec(memory_space=pltpu.VMEM), pl.BlockSpec(memory_space=pl.ANY)
    return pl.pallas_call(
        functools.partial(layers_kernel, sections, width),
        out_shape=[
            jax.ShapeDtypeStruct((micro, local, features), bf16),
            jax.ShapeDtypeStruct((shares, block, rank), bf16),
        ],
        in_specs=[pl.BlockSpec(memory_space=pltpu.SMEM), inside, inside] + [outside] * 3,
        out_specs=[inside, inside],
        scratch_shapes=[
            pltpu.VMEM(joined.shape, bf16),
            pltpu.VMEM(proj.shape, bf16),
            pltpu.VMEM(up.shape, bf16),
            pltpu.VMEM((sections - 1, rows, features), bf16),
            pltpu.VMEM((sections, rows, features), bf16),
            pltpu.VMEM((sections, rows, rank), bf16),
            pltpu.VMEM((sections, rows, width + rank), bf16),
            pltpu.VMEM((rows, features), f32),
            pltpu.VMEM((sections, rows, features), bf16),
            pltpu.VMEM((rows, width + rank), f32),
            pltpu.SemaphoreType.DMA((sections * 3,)),
        ],
        compiler_params=pltpu.CompilerParams(vmem_limit_bytes=56 * 2**20),
    )(order, tokens.reshape(rows, features), cotangent.reshape(rows, features), joined, proj, up)


def custom_route():
    fsdp = lax.axis_size("fsdp")
    return lax.axis_size("section") == 2 and fsdp % 4 == 0 and fsdp <= 16


def gather_weights(w_value, w_out, adapter_down, adapter_up):
    sections = lax.axis_size("section")
    joined = jnp.concatenate([w_value[0], adapter_down[0]], axis=1)
    proj = w_out[0].T
    up = adapter_up[0].T

    if custom_route():
        return tuple(
            full.reshape(sections, -1, full.shape[2]) for full in spread(joined, proj, up)
        )

    def whole(block):
        full = lax.all_gather(block, ("section", "fsdp"), axis=0, tiled=True)
        return full.reshape(sections, -1, block.shape[1])

    return whole(joined), whole(proj), whole(up)


def body(tokens, cotangent, order, w_value, w_out, adapter_down, adapter_up):
    sections = lax.axis_size("section")
    position = lax.axis_index("section")
    micro, local, features = tokens.shape
    width = w_value.shape[2]
    joined, proj, up = gather_weights(w_value, w_out, adapter_down, adapter_up)

    if custom_route():
        out, parts = run_layers(tokens, cotangent, order, joined, proj, up)
        shares = lax.axis_size("fsdp")
        grad_down, grad_up = settle(
            parts.reshape(shares // 2, 2, *parts.shape[1:]), features // shares
        )
        return (out[None], grad_down[None], grad_up.T[None])

    current = tokens.reshape(micro * local, features)
    saved = []
    for layer in range(sections):
        widened = current.astype(jnp.float32)
        inverse = lax.rsqrt(jnp.mean(widened * widened, axis=-1, keepdims=True) + epsilon)
        normed = (widened * inverse).astype(jnp.bfloat16)
        last = layer == sections - 1
        if last:
            low = widen_dot(normed, joined[layer][:, width:]).astype(jnp.bfloat16)
        else:
            both = widen_dot(normed, joined[layer])
            low = both[:, width:].astype(jnp.bfloat16)
            values = (both[:, :width] + widen_dot(low, up[layer], ((1,), (1,)))).astype(jnp.bfloat16)
        saved.append((current, normed, low, inverse))
        if not last:
            current = (widened + widen_dot(values, proj[layer], ((1,), (1,)))).astype(jnp.bfloat16)

    upstream = cotangent.reshape(micro * local, features)
    grads, d_vals, d_lows = [], [], []
    for layer in reversed(range(sections)):
        inputs, normed, low, inverse = saved[layer]
        d_values = widen_dot(upstream, proj[layer]).astype(jnp.bfloat16)
        d_low = widen_dot(d_values, up[layer]).astype(jnp.bfloat16)
        d_normed = widen_dot(
            jnp.concatenate([d_values, d_low], axis=1), joined[layer], ((1,), (1,))
        )
        widened = inputs.astype(jnp.float32)
        project = jnp.mean(d_normed * widened, axis=-1, keepdims=True)
        upstream = (
            upstream.astype(jnp.float32)
            + inverse * (d_normed - widened * inverse * inverse * project)
        ).astype(jnp.bfloat16)
        grads.insert(0, upstream)
        d_vals.insert(0, d_values)
        d_lows.insert(0, d_low)

    def mine(items):
        chosen = items[0]
        for layer in range(1, sections):
            chosen = jnp.where(position == layer, items[layer], chosen)
        return chosen

    shares = lax.axis_size("fsdp")
    normed = mine([item[1] for item in saved])
    low = mine([item[2] for item in saved])
    part_down = widen_dot(normed, mine(d_lows), ((0,), (0,)))
    part_up = widen_dot(mine(d_vals), low, ((0,), (0,)))
    rank = low.shape[1]
    parts = jnp.concatenate(
        [part_down.reshape(shares, -1, rank), part_up.reshape(shares, -1, rank)], axis=1
    )
    share_down = features // shares
    combined = lax.psum_scatter(parts, "fsdp", scatter_dimension=0, tiled=True)[0]
    grad_down, grad_up = combined[:share_down], combined[share_down:]
    out = mine(grads).reshape(micro, local, features)[order]
    return (out[None], grad_down[None], grad_up.T[None])


def solution(mesh):
    return jax.shard_map(
        body,
        mesh=mesh,
        in_specs=(
            P(None, "fsdp", None),
            P(None, "fsdp", None),
            P(),
            P("section", "fsdp", None),
            P("section", None, "fsdp"),
            P("section", "fsdp", None),
            P("section", None, "fsdp"),
        ),
        out_specs=(
            P("section", None, "fsdp", None),
            P("section", "fsdp", None),
            P("section", None, "fsdp"),
        ),
        check_vma=False,
    )
```

profile of v0, /device:TPU:0, one launch (start us, length us, event | category | flops | bytes accessed | tf_op | source)
XLA Modules:
  0.0 137.1 jit_solution(14443482927655761916)
XLA Ops:
  0.6 1.8 %copy.10 = bf16[1,512,256]{1,2,0:T(8,128)(2,1)} copy(bf16[1,512,256]{2,1,0:T(8,128)(2,1)} %param.11) | data formatting | bytes 524288 | tf_op args[4]
  2.4 1.7 %pad_maximum_fusion.a_ref = bf16[256,640]{1,0:T(8,128)(2,1)} fusion(bf16[256,128]{1,0:T(8,128)(2,1)} %bitcast.28, bf16[256,512]{1,0:T(8,128)(2,1)} %bitcast.26), kind=kLoop, calls=%fused_computation | loop fusion | flops 655360 | bytes 655360 | tf_op jit(solution)/shard_map/concatenate | solution.py:416
  4.2 80.6 %shard_map.94 = (bf16[32,256,640]{2,1,0:T(8,128)(2,1)}, bf16[32,256,512]{2,1,0:T(8,128)(2,1)}, bf16[32,32,128]{2,1,0:T(8,128)(2,1)}) custom-call(bf16[256,640]{1,0:T(8,128)(2,1)} %pad_maximum_fusion.a_ref, bf16[256,512]{1,0:T(8,128)(2,1)} %bitcast.24, bf16[32,128]{1,0:T(8,128)(2,1)} %bitcast.30), custom_call_target="tpu_custom_call" | custom-call | tf_op jit(solution)/shard_map/pallas_call | solution.py:159
  84.8 32.2 %shard_map.95 = (bf16[6,32,4096]{2,1,0:T(8,128)(2,1)}, bf16[16,288,128]{2,1,0:T(8,128)(2,1)}) custom-call(s32[6]{0:T(128)} %order_ref.1, bf16[192,4096]{1,0:T(8,128)(2,1)} %bitcast.21, bf16[192,4096]{1,0:T(8,128)(2,1)} %bitcast.22, bf16[2,4096,640]{2,1,0:T(8,128)(2,1)} %bitcast.19, bf16[2,4096,512]{2,1,0:T(8,128)(2,1)} %bitcast.20, bf16[2,512,128]{2,1,0:T(8,128)(2,1)} %bitcast.25), custom_call_target="tpu_custom_call" | custom-call | tf_op jit(solution)/shard_map/pallas_call | solution.py:384
  117.0 17.2 %shard_map.96 = (f32[256,128]{1,0:T(8,128)}, f32[32,128]{1,0:T(8,128)}) custom-call(bf16[8,2,288,128]{3,2,1,0:T(8,128)(2,1)} %bitcast.23), custom_call_target="tpu_custom_call" | custom-call | tf_op jit(solution)/shard_map/pallas_call | solution.py:230
  134.2 1.6 %copy.13 = f32[1,256,128]{2,1,0:T(8,128)} copy(f32[1,256,128]{2,1,0:T(8,128)} %bitcast.27) | data formatting | bytes 262144
  135.7 1.3 copy.14
where the time goes:
time: 138 us; the launch traced here: 137 us
  Pallas kernels  130 us (94%)
  local copies, waits for them, and re-layouts  4.7 us (3%)
  other arithmetic  1.74 us (1%)
    pallas_call x1, Pallas kernels, spread(): pl.pallas_call(functools.partial(spread_kernel, fsdp // 4, plan), out_sha...  80.6 us
    pallas_call x1, Pallas kernels, run_layers(): pl.pallas_call(functools.partial(layers_kernel, sections, width), out_sha...  32.2 us
    pallas_call x1, Pallas kernels, settle(): pl.pallas_call(settle_kernel, out_shape=[jax.ShapeDtypeStruct((split, ran...  17.2 us
    unnamed x3, local copies, waits for them, and re-layouts  4.7 us

commit v1 on v0

v1 whole, which is shorter than its diff:
```python
import functools

import jax
import jax.numpy as jnp
from jax import lax
from jax.experimental import pallas as pl
from jax.experimental.pallas import tpu as pltpu
from jax.sharding import PartitionSpec as P

epsilon = 1e-05
MESH = pl.DeviceIdType.MESH
X, Y, Z = 0, 1, 2
OUT, MIX, UP = 0, 1, 2
bf16, f32 = jnp.bfloat16, jnp.float32


def widen_dot(left, right, dims=((1,), (0,))):
    return lax.dot_general(left, right, (dims, ((), ())), preferred_element_type=f32)


def plan_of(out_rows, mix_rows, up_rows):
    out_y, mix_y, mix_x = out_rows * 3 // 16, mix_rows // 8, mix_rows // 4
    out_z, mix_z = (out_rows - out_y) // 2, (mix_rows - mix_y - mix_x) // 2
    return (
        (UP, 0, up_rows, (Z, Y)),
        (OUT, 0, out_z, (Z, Y, X)),
        (OUT, 2 * out_z, out_y, (Y, Z, X)),
        (OUT, out_z, out_z, (Z, Y, X)),
        (MIX, 0, mix_z, (Z, Y, X)),
        (MIX, mix_z, mix_z, (Z, Y, X)),
        (MIX, 2 * mix_z, mix_y, (Y, Z, X)),
        (MIX, 2 * mix_z + mix_y, mix_x, (X, Z, Y)),
    )


def relay_kernel(
    lines, plan, tok_any, cot_any, value_any, down_any, out_any, up_any, flow_any, grad_any,
    mix, out, up, tok, cot, normed, states, wide, flow, acc, vals, cats, tail, low, squares, products, scales,
    parts, near, mine, far, total,
    local_sem, recv_sem, send_sem, swap_recv, swap_send, near_recv, near_send, far_recv, far_send,
):
    pieces = len(plan)
    rows, features = tok.shape
    width = vals.shape[1]
    fsdp = lines * 4
    chips = lines * 2
    block = features // fsdp
    sheet = block * 4
    share_up = up.shape[1]
    s, f = lax.axis_index("section"), lax.axis_index("fsdp")
    core, y, z = f % 2, (f // 2) % 2, f // 4
    chip = f // 2
    first, second = s == 0, s == 1

    def place(s_, z_, y_, c_):
        return {"section": s_, "fsdp": (z_ * 2 + y_) * 2 + c_}

    partner = place(s, z, y, 1 - core)
    across = place(1 - s, z, y, core)
    beside = place(s, z, 1 - y, core)
    above = place(s, z + 1, y, core)
    below = place(s, z - 1, y, core)

    def stage(source, target, index):
        copy = pltpu.make_async_copy(source, target, local_sem.at[index])
        copy.start()
        return copy

    def band(slot, start, count):
        return pl.ds(pl.multiple_of(slot * block + start, 16), count)

    staged = {
        UP: [stage(up_any, up.at[f], 0)],
        OUT: [stage(out_any, out.at[s, f], 1)],
        MIX: [
            stage(value_any, mix.at[s, band(f, 0, block), :width], 2),
            stage(down_any, mix.at[s, band(f, 0, block), width:], 3),
        ],
    }
    tok_copy, cot_copy = stage(tok_any, tok, 4), stage(cot_any, cot, 5)

    barrier = pltpu.get_barrier_semaphore()
    for target in (partner, across):
        pl.semaphore_signal(barrier, inc=1, device_id=target, device_id_type=MESH)
    for step in range(1, chips):
        target = {"section": s, "fsdp": ((chip + step) % chips) * 2 + core}
        pl.semaphore_signal(barrier, inc=1, device_id=target, device_id_type=MESH)
    pl.semaphore_wait(barrier, chips + 1)

    def when(test, action):
        if test is True:
            action()
        else:
            pl.when(test)(action)

    def both(left, right):
        return right if left is True else left if right is True else left & right

    def slot_of(dy, dz, c_):
        return ((z + dz) * 2 + (y + dy) % 2) * 2 + c_

    def piece(index, owner, slot):
        array, start, count, _ = plan[index]
        if array == MIX:
            return mix.at[owner, band(slot, start, count), :]
        if array == OUT:
            return out.at[owner, slot, pl.ds(start, count)]
        return up.at[slot, pl.ds(start, count)]

    def inside(dz):
        return True if dz == 0 else (z + dz < lines) if dz > 0 else (z + dz >= 0)

    def gets(index, dx):
        if not dx:
            return True
        return first if plan[index][0] == MIX else second

    def gives(index):
        return second if plan[index][0] == MIX else first

    def sem_of(index, dx, slot):
        return recv_sem.at[(dx * fsdp + slot) * pieces + index]

    def sends(index, dx, dy, dz):
        order = plan[index][3]
        slot, owner = slot_of(dy, dz, core), (s + dx) % 2
        step = ((dx * 2 + dy) * lines + dz % lines) * pieces + index
        gone = {X: dx != 0, Y: dy != 0, Z: dz != 0}
        here = piece(index, owner, slot)
        result = []

        def add(way, test, target, hop=0):
            copy = pltpu.make_async_remote_copy(
                src_ref=here,
                dst_ref=here,
                send_sem=send_sem.at[step * 5 + way],
                recv_sem=sem_of(index, (dx + hop) % 2, slot),
                device_id=target,
                device_id_type=MESH,
            )
            result.append((test, copy))

        for rank, dim in enumerate(order):
            if any(gone[later] for later in order[rank + 1:]):
                continue
            if dim == Z:
                if dz <= 0:
                    add(0, z + 1 < lines, above)
                if dz >= 0:
                    add(1, z > 0, below)
            elif dim == Y and not gone[Y]:
                add(2, True, beside)
            elif dim == X and not gone[X]:
                add(3, gives(index), across, 1)
        add(4, True, partner)
        return result

    def arrived(index, dx, slot):
        ref = piece(index, (s + dx) % 2, slot)
        pltpu.make_async_copy(ref, ref, sem_of(index, dx, slot)).wait()

    levels = {}
    for dx in (0, 1):
        for dy in (0, 1):
            for dz in range(1 - lines, lines):
                for index in range(pieces):
                    if X in plan[index][3] or not dx:
                        levels.setdefault(dx + dy + abs(dz), []).append((index, dx, abs(dz), dy, dz))
    for level in levels.values():
        level.sort()
    of = {array: [index for index in range(pieces) if plan[index][0] == array] for array in (OUT, MIX, UP)}

    def relay(index, dx, dy, dz):
        def action():
            if dx or dy or dz:
                arrived(index, dx, slot_of(dy, dz, core))
            else:
                for copy in staged.pop(plan[index][0], ()):
                    copy.wait()
            for test, copy in sends(index, dx, dy, dz):
                when(test, copy.start)

        when(both(inside(dz), gets(index, dx)), action)

    def level_relays(distance):
        for index, dx, _, dy, dz in levels[distance]:
            relay(index, dx, dy, dz)

    turned = z // (lines // 2)
    folded = z + turned * (lines - 1 - 2 * z)

    def plane_of(rank):
        near_plane = folded if rank == 0 else 1 - folded if rank == 1 else rank
        return near_plane + turned * (lines - 1 - 2 * near_plane)

    def partners_arrived(array, dx, plane):
        for y_ in (0, 1):
            for index in of[array]:
                arrived(index, dx, (plane * 2 + y_) * 2 + 1 - core)

    def columns(index, count):
        return pl.ds(pl.multiple_of(index * count, count), count)

    def fold(product):
        sums = product[:, :128]
        for start in range(128, product.shape[1], 128):
            sums = sums + product[:, start:start + 128]
        return sums

    step = width

    def blocks(action, size=step):
        def run(index, carry):
            action(index)
            return carry

        lax.fori_loop(0, features // size, run, 0)

    def mean_of(sums):
        return jnp.sum(sums[...], axis=1, keepdims=True) / features

    level_relays(0)
    acc[...] = jnp.zeros_like(acc)
    squares[...] = jnp.zeros_like(squares)
    tok_copy.wait()
    cot_copy.wait()

    @pl.when(first)
    def _():
        def square(index):
            entries = tok[:, columns(index, step)].astype(f32)
            squares[...] += fold(entries * entries)

        blocks(square)
        inverse = lax.rsqrt(mean_of(squares) + epsilon)

        def scale(index):
            span = columns(index, step)
            normed[:, span] = (tok[:, span].astype(f32) * inverse).astype(bf16)

        blocks(scale)
        scales[...] = jnp.broadcast_to(inverse, scales.shape)

    for rank in range(lines):
        level_relays(rank + 1)
        plane = plane_of(rank)

        @pl.when(first)
        def _():
            partners_arrived(MIX, 0, plane)
            span = columns(plane, sheet)
            acc[...] += widen_dot(normed[:, span], mix[0, span, :])

        @pl.when(second)
        def _():
            partners_arrived(OUT, 0, plane)
            sums = acc[:, :width]
            for part in range(4):
                span = pl.ds(pl.multiple_of(plane * sheet + part * block, block), block)
                sums = sums + widen_dot(cot[:, span], out[1, plane * 4 + part], ((1,), (1,)))
            acc[:, :width] = sums

    for plane in range(lines):
        partners_arrived(UP, 0, plane)

    def swap(ref, index):
        return pltpu.make_async_remote_copy(
            src_ref=ref,
            dst_ref=ref,
            send_sem=swap_send.at[index],
            recv_sem=swap_recv.at[index],
            device_id=across,
            device_id_type=MESH,
        )

    def ups():
        return up[...].reshape(fsdp * share_up, up.shape[2])

    @pl.when(first)
    def _():
        low[...] = acc[:, width:].astype(bf16)
        vals[...] = (acc[:, :width] + widen_dot(low[...], ups(), ((1,), (1,)))).astype(bf16)
        swap(vals, 0).start()

    @pl.when(second)
    def _():
        cats[:, :width] = acc[:, :width].astype(bf16)
        cats[:, width:] = widen_dot(cats[:, :width], ups()).astype(bf16)
        swap(cats, 1).start()

    level_relays(lines + 1)

    @pl.when(first)
    def _():
        for plane in range(lines):
            partners_arrived(OUT, 0, plane)

    @pl.when(second)
    def _():
        for plane in range(lines):
            partners_arrived(OUT, 1, plane)
        swap(vals, 0).wait_recv()

    squares[...] = jnp.zeros_like(squares)
    products[...] = jnp.zeros_like(products)

    def widen(index):
        span = columns(index, block)
        entries = (tok[:, span].astype(f32) + widen_dot(vals[...], out[0, index])).astype(bf16)
        states[:, span] = entries
        back = entries.astype(f32)
        squares[...] += fold(back * back)

    blocks(widen, block)

    @pl.when(first)
    def _():
        for plane in range(lines):
            partners_arrived(MIX, 1, plane)
        swap(cats, 1).wait_recv()

    @pl.when(second)
    def _():
        for plane in range(lines):
            partners_arrived(MIX, 0, plane)

    def open_up(layer, joint, inputs):
        def action(index):
            span = columns(index, step)
            entries = widen_dot(joint[...], mix[layer, span, :], ((1,), (1,)))
            wide[:, span] = entries
            products[...] += fold(entries * inputs[:, span].astype(f32))

        blocks(action)

    open_up(1, cats, states)
    inverse = lax.rsqrt(mean_of(squares) + epsilon)
    factor = inverse * inverse * mean_of(products)
    acc[...] = jnp.zeros_like(acc)

    def gradients(joint):
        def contract(index, carry):
            parts[index // 2, index % 2, :block, :] = widen_dot(
                normed[:, columns(index, block)], joint[:, width:], ((0,), (0,))
            ).astype(bf16)
            return carry

        lax.fori_loop(0, fsdp, contract, 0)
        ends = widen_dot(joint[:, :width], low[...], ((0,), (0,))).astype(bf16)
        for index in range(fsdp):
            parts[index // 2, index % 2, block:, :] = ends[index * share_up:(index + 1) * share_up]

    def upstream_of(span):
        inputs = states[:, span].astype(f32)
        entries = cot[:, span].astype(f32) + inverse * (wide[:, span] - inputs * factor)
        flow[:, span] = entries.astype(bf16)
        return inputs

    @pl.when(first)
    def _():
        def narrow(index):
            span = columns(index, block)
            upstream_of(span)
            acc[:, :width] += widen_dot(flow[:, span], out[0, index], ((1,), (1,)))

        blocks(narrow, block)
        tail[:, :width] = acc[:, :width].astype(bf16)
        tail[:, width:] = widen_dot(tail[:, :width], ups()).astype(bf16)
        gradients(tail)

    @pl.when(second)
    def _():
        def lower(index):
            span = columns(index, step)
            inputs = upstream_of(span)
            normed[:, span] = (inputs * inverse).astype(bf16)
            acc[:, width:] += widen_dot(normed[:, span], mix[1, span, width:])

        blocks(lower)
        low[...] = acc[:, width:].astype(bf16)
        gradients(cats)

    handed, passed = [], []
    for turn in range(chips):
        target = (chip + 1 + turn) % chips
        copy = pltpu.make_async_remote_copy(
            src_ref=parts.at[target, 1 - core],
            dst_ref=near.at[turn],
            send_sem=near_send.at[turn],
            recv_sem=near_recv.at[turn],
            device_id=partner,
            device_id_type=MESH,
        )
        copy.start()
        handed.append(copy)
    for turn in range(chips - 1):
        target = (chip + 1 + turn) % chips
        handed[turn].wait_recv()
        mine[turn] = (parts[target, core].astype(f32) + near[turn].astype(f32)).astype(bf16)
        copy = pltpu.make_async_remote_copy(
            src_ref=mine.at[turn],
            dst_ref=far.at[turn],
            send_sem=far_send.at[turn],
            recv_sem=far_recv.at[turn],
            device_id={"section": s, "fsdp": target * 2 + core},
            device_id_type=MESH,
        )
        passed.append(copy)
        if turn:
            passed[turn - 1].start()
    handed[-1].wait_recv()
    total[...] = parts[chip, core].astype(f32) + near[chips - 1].astype(f32)
    passed[-1].start()

    @pl.when(first)
    def _():
        products[...] = jnp.zeros_like(products)
        open_up(0, tail, tok)
        inverse = scales[:, :1]
        factor = inverse * inverse * mean_of(products)

        def finish(index):
            span = columns(index, step)
            entries = flow[:, span].astype(f32) + inverse * (wide[:, span] - tok[:, span].astype(f32) * factor)
            flow[:, span] = entries.astype(bf16)

        blocks(finish)

    flow_copy = pltpu.make_async_copy(flow, flow_any, local_sem.at[0])
    flow_copy.start()
    for turn in range(chips - 1):
        passed[turn].wait_recv()
        total[...] += far[turn].astype(f32)
    grad_copy = pltpu.make_async_copy(total, grad_any, local_sem.at[1])
    grad_copy.start()
    for distance in sorted(levels):
        for index, dx, _, dy, dz in levels[distance]:
            for test, copy in sends(index, dx, dy, dz):
                when(both(both(inside(dz), gets(index, dx)), test), copy.wait_send)
    pl.when(first)(swap(vals, 0).wait_send)
    pl.when(second)(swap(cats, 1).wait_send)
    for copy in handed + passed:
        copy.wait_send()
    flow_copy.wait()
    grad_copy.wait()


def finish_kernel(micro, order_ref, flow_ref, grad_ref, out_ref, down_ref, up_ref):
    local = flow_ref.shape[0] // micro
    for slot in range(micro):
        out_ref[slot] = flow_ref[pl.ds(pl.multiple_of(order_ref[slot] * local, local), local), :]
    split = down_ref.shape[0]
    down_ref[...] = grad_ref[:split]
    up_ref[...] = grad_ref[split:]


def custom_route():
    fsdp = lax.axis_size("fsdp")
    return lax.axis_size("section") == 2 and fsdp % 8 == 0 and fsdp <= 16


def run_custom(tokens, cotangent, order, value, down, out, up):
    micro, local, features = tokens.shape
    rows = micro * local
    fsdp = lax.axis_size("fsdp")
    lines, chips = fsdp // 4, fsdp // 2
    block, width = value.shape
    rank = down.shape[1]
    share_up = up.shape[0]
    both, high = width + rank, block + share_up
    plan = plan_of(width, block, share_up)
    pieces = len(plan)
    outside, inside = pl.BlockSpec(memory_space=pl.ANY), pl.BlockSpec(memory_space=pltpu.VMEM)
    dma = pltpu.SemaphoreType.DMA
    vmem = pltpu.VMEM
    flow, grads = pl.pallas_call(
        functools.partial(relay_kernel, lines, plan),
        out_shape=[
            jax.ShapeDtypeStruct((rows, features), bf16),
            jax.ShapeDtypeStruct((high, rank), f32),
        ],
        in_specs=[outside] * 6,
        out_specs=[outside] * 2,
        scratch_shapes=[
            vmem((2, features, both), bf16),
            vmem((2, fsdp, width, block), bf16),
            vmem((fsdp, share_up, rank), bf16),
            vmem((rows, features), bf16),
            vmem((rows, features), bf16),
            vmem((rows, features), bf16),
            vmem((rows, features), bf16),
            vmem((rows, features), f32),
            vmem((rows, features), bf16),
            vmem((rows, both), f32),
            vmem((rows, width), bf16),
            vmem((rows, both), bf16),
            vmem((rows, both), bf16),
            vmem((rows, rank), bf16),
            vmem((rows, 128), f32),
            vmem((rows, 128), f32),
            vmem((rows, 128), f32),
            vmem((chips, 2, high, rank), bf16),
            vmem((chips, high, rank), bf16),
            vmem((chips, high, rank), bf16),
            vmem((chips, high, rank), bf16),
            vmem((high, rank), f32),
            dma((6,)),
            dma((2 * fsdp * pieces,)),
            dma((fsdp * pieces * 5,)),
            dma((2,)),
            dma((2,)),
            dma((chips,)),
            dma((chips,)),
            dma((chips,)),
            dma((chips,)),
        ],
        compiler_params=pltpu.CompilerParams(
            collective_id=0, has_side_effects=True, vmem_limit_bytes=52 * 2**20
        ),
    )(tokens.reshape(rows, features), cotangent.reshape(rows, features), value, down, out, up)
    return pl.pallas_call(
        functools.partial(finish_kernel, micro),
        out_shape=[
            jax.ShapeDtypeStruct((micro, local, features), bf16),
            jax.ShapeDtypeStruct((block, rank), f32),
            jax.ShapeDtypeStruct((share_up, rank), f32),
        ],
        in_specs=[pl.BlockSpec(memory_space=pltpu.SMEM), inside, inside],
        out_specs=[inside] * 3,
    )(order, flow, grads)


def gather_weights(w_value, w_out, adapter_down, adapter_up):
    sections = lax.axis_size("section")

    def whole(block):
        full = lax.all_gather(block, ("section", "fsdp"), axis=0, tiled=True)
        return full.reshape(sections, -1, block.shape[1])

    joined = jnp.concatenate([w_value[0], adapter_down[0]], axis=1)
    return whole(joined), whole(w_out[0].T), whole(adapter_up[0].T)


def body(tokens, cotangent, order, w_value, w_out, adapter_down, adapter_up):
    sections = lax.axis_size("section")
    position = lax.axis_index("section")
    micro, local, features = tokens.shape
    width = w_value.shape[2]

    if custom_route():
        out, grad_down, grad_up = run_custom(
            tokens, cotangent, order, w_value[0], adapter_down[0], w_out[0], adapter_up[0].T
        )
        return (out[None], grad_down[None], grad_up.T[None])

    joined, proj, up = gather_weights(w_value, w_out, adapter_down, adapter_up)
    current = tokens.reshape(micro * local, features)
    saved = []
    for layer in range(sections):
        widened = current.astype(jnp.float32)
        inverse = lax.rsqrt(jnp.mean(widened * widened, axis=-1, keepdims=True) + epsilon)
        normed = (widened * inverse).astype(jnp.bfloat16)
        last = layer == sections - 1
        if last:
            low = widen_dot(normed, joined[layer][:, width:]).astype(jnp.bfloat16)
        else:
            both = widen_dot(normed, joined[layer])
            low = both[:, width:].astype(jnp.bfloat16)
            values = (both[:, :width] + widen_dot(low, up[layer], ((1,), (1,)))).astype(jnp.bfloat16)
        saved.append((current, normed, low, inverse))
        if not last:
            current = (widened + widen_dot(values, proj[layer], ((1,), (1,)))).astype(jnp.bfloat16)

    upstream = cotangent.reshape(micro * local, features)
    grads, d_vals, d_lows = [], [], []
    for layer in reversed(range(sections)):
        inputs, normed, low, inverse = saved[layer]
        d_values = widen_dot(upstream, proj[layer]).astype(jnp.bfloat16)
        d_low = widen_dot(d_values, up[layer]).astype(jnp.bfloat16)
        d_normed = widen_dot(
            jnp.concatenate([d_values, d_low], axis=1), joined[layer], ((1,), (1,))
        )
        widened = inputs.astype(jnp.float32)
        project = jnp.mean(d_normed * widened, axis=-1, keepdims=True)
        upstream = (
            upstream.astype(jnp.float32)
            + inverse * (d_normed - widened * inverse * inverse * project)
        ).astype(jnp.bfloat16)
        grads.insert(0, upstream)
        d_vals.insert(0, d_values)
        d_lows.insert(0, d_low)

    def mine(items):
        chosen = items[0]
        for layer in range(1, sections):
            chosen = jnp.where(position == layer, items[layer], chosen)
        return chosen

    shares = lax.axis_size("fsdp")
    normed = mine([item[1] for item in saved])
    low = mine([item[2] for item in saved])
    part_down = widen_dot(normed, mine(d_lows), ((0,), (0,)))
    part_up = widen_dot(mine(d_vals), low, ((0,), (0,)))
    rank = low.shape[1]
    parts = jnp.concatenate(
        [part_down.reshape(shares, -1, rank), part_up.reshape(shares, -1, rank)], axis=1
    )
    share_down = features // shares
    combined = lax.psum_scatter(parts, "fsdp", scatter_dimension=0, tiled=True)[0]
    grad_down, grad_up = combined[:share_down], combined[share_down:]
    out = mine(grads).reshape(micro, local, features)[order]
    return (out[None], grad_down[None], grad_up.T[None])


def solution(mesh):
    return jax.shard_map(
        body,
        mesh=mesh,
        in_specs=(
            P(None, "fsdp", None),
            P(None, "fsdp", None),
            P(),
            P("section", "fsdp", None),
            P("section", None, "fsdp"),
            P("section", "fsdp", None),
            P("section", None, "fsdp"),
        ),
        out_specs=(
            P("section", None, "fsdp", None),
            P("section", "fsdp", None),
            P("section", None, "fsdp"),
        ),
        check_vma=False,
    )
```

time: 138 us -> 109 us (0.79)
  the two profiles are of different devices: /device:TPU:0 before, /device:TPU:15 now
where the time goes in v1:
time: 109 us
  Pallas kernels  104 us (95%)
  local copies, waits for them, and re-layouts  4.08 us (4%)
    pallas_call x1, Pallas kernels, run_custom(): pl.pallas_call(functools.partial(relay_kernel, lines, plan), out_shape=[j...  101 us
    unnamed x10, local copies, waits for them, and re-layouts  4.08 us
    pallas_call x1, Pallas kernels, run_custom(): pl.pallas_call(functools.partial(finish_kernel, micro), out_shape=[jax.Sh...  2.71 us

profile of v1, /device:TPU:15, one launch (start us, length us, event | category | flops | bytes accessed | tf_op | source)
XLA Modules:
  0.0 108.7 jit_solution(10000938061803259671)
XLA Ops:
  0.6 0.0 copy-start
  0.6 0.9 copy-done
  1.6 0.0 copy-start.1
  1.6 0.9 copy-done.1
  2.5 0.0 copy-start.3
  2.5 0.8 copy-done.3
  3.4 0.0 copy-start.4
  3.4 0.7 copy-done.4
  4.1 101.2 %shard_map.94 = (bf16[192,4096]{1,0:T(8,128)(2,1)}, f32[288,128]{1,0:T(8,128)S(1)}) custom-call(bf16[192,4096]{1,0:T(8,128)(2,1)} %bitcast.17, bf16[192,4096]{1,0:T(8,128)(2,1)} %bitcast.18, bf16[256,512]{1,0:T(8,128)(2,1)S(1)} %bitcast.13, bf16[256,128]{1,0:T(8,128)(2,1)S(1)} %bitcast.15, bf16[512,256]{1,0:T(8,128)(2,1)S(1)} %bitcast.14, ...), custom_call_target="tpu_custom_call" | custom-call | tf_op jit(solution)/shard_map/pallas_call | solution.py:476
  105.3 0.0 copy-start.2
  105.3 0.6 copy-done.2
  106.0 2.7 %shard_map.95 = (bf16[6,32,4096]{2,1,0:T(8,128)(2,1)}, f32[256,128]{1,0:T(8,128)}, f32[32,128]{1,0:T(8,128)}) custom-call(s32[6]{0:T(128)} %order_ref.1, bf16[192,4096]{1,0:T(8,128)(2,1)} %get-tuple-element.8.flow_ref, f32[288,128]{1,0:T(8,128)} %copy-done.2), custom_call_target="tpu_custom_call" | custom-call | tf_op jit(solution)/shard_map/pallas_call | solution.py:521
Async XLA Ops:
  0.6 1.0 copy-start
  1.6 0.9 copy-start.1
  2.5 0.8 copy-start.3
  3.4 0.7 copy-start.4
  105.3 0.7 copy-start.2

commit v2 on v1

v2 whole, which is shorter than its diff:
```python
import functools

import jax
import jax.numpy as jnp
from jax import lax
from jax.experimental import pallas as pl
from jax.experimental.pallas import tpu as pltpu
from jax.sharding import PartitionSpec as P

epsilon = 1e-05
MESH = pl.DeviceIdType.MESH
X, Y, Z = 0, 1, 2
OUT, MIX, UP = 0, 1, 2
bf16, f32 = jnp.bfloat16, jnp.float32


def widen_dot(left, right, dims=((1,), (0,))):
    return lax.dot_general(left, right, (dims, ((), ())), preferred_element_type=f32)


def plan_of(out_rows, mix_rows, up_rows):
    def cut(array, rows, shares):
        start, result = 0, []
        for share, order, late in shares:
            count = rows * share // 32
            result.append((array, start, count, order, late))
            start += count
        return result

    none = ((0, 0), (0, 0))
    return tuple(
        cut(UP, up_rows, [(32, (Z, Y), none)])
        + cut(OUT, out_rows, [
                (7, (Z, Y, X), ((-0.25, -1.0), (-0.25, 2.0))),
                (10, (Z, Y, X), ((0, 0.25), (0, 0.0))),
                (8, (Y, Z, X), ((0.5, 0), (-0.75, 1.25))),
                (7, (X, Z, Y), ((2, -1.5), (0.25, 1.75))),
            ])
        + cut(MIX, mix_rows, [
                (8, (Z, Y, X), ((-0.5, 2.5), (0.75, 1.25))),
                (16, (Z, Y, X), ((0.25, -0.5), (-1, 0.75))),
                (4, (X, Z, Y), ((0, 1.5), (1.5, 2.0))),
                (4, (X, Y, Z), ((-0.25, 2), (2, -1))),
            ])
    )


def relay_kernel(
    lines, plan, tok_any, cot_any, value_any, down_any, out_any, up_any, flow_any, grad_any,
    mix, out, up, tok, cot, normed, states, wide, flow, acc, vals, cats, tail, low, squares, products, scales,
    parts, near, mine, beside_sums, sent, far, total,
    local_sem, recv_sem, send_sem, swap_sem, near_sem, side_sem, far_sem,
):
    pieces = len(plan)
    rows, features = tok.shape
    width, rank = vals.shape[1], low.shape[1]
    fsdp, chips = lines * 4, lines * 2
    block = features // fsdp
    sheet = block * 4
    share_up = up.shape[0] // fsdp
    high = {UP: share_up, OUT: width, MIX: block}
    count_of = {array: sum(item[0] == array for item in plan) for array in high}
    lead = {array: min(index for index in range(pieces) if plan[index][0] == array) for array in high}
    kinds = pieces + max(count_of[OUT], count_of[MIX])
    s, f = lax.axis_index("section"), lax.axis_index("fsdp")
    core, y, z = f % 2, (f // 2) % 2, f // 4
    chip = f // 2

    def place(s_, z_, y_, c_):
        return {"section": s_, "fsdp": (z_ * 2 + y_) * 2 + c_}

    partner = place(s, z, y, 1 - core)
    across = place(1 - s, z, y, core)
    beside = place(s, z, 1 - y, core)
    above = place(s, z + 1, y, core)
    below = place(s, z - 1, y, core)

    def stage(source, target, index):
        copy = pltpu.make_async_copy(source, target, local_sem.at[index])
        copy.start()
        return copy

    def band(array, slot, start, count):
        return pl.ds(pl.multiple_of(slot * high[array] + start, 16), count)

    staged = {
        UP: [stage(up_any, up.at[band(UP, f, 0, share_up), :], 0)],
        OUT: [stage(out_any, out.at[s, band(OUT, f, 0, width), :], 1)],
        MIX: [
            stage(value_any, mix.at[s, band(MIX, f, 0, block), :width], 2),
            stage(down_any, mix.at[s, band(MIX, f, 0, block), width:], 3),
        ],
    }
    inputs_staged = [stage(tok_any, tok, 4), stage(cot_any, cot, 5)]

    barrier = pltpu.get_barrier_semaphore()
    for target in (partner, across):
        pl.semaphore_signal(barrier, inc=1, device_id=target, device_id_type=MESH)
    for step in range(1, chips):
        target = {"section": s, "fsdp": ((chip + step) % chips) * 2 + core}
        pl.semaphore_signal(barrier, inc=1, device_id=target, device_id_type=MESH)
    pl.semaphore_wait(barrier, chips + 1)
    for array in (UP, OUT, MIX):
        for copy in staged[array]:
            copy.wait()

    def when(test, action):
        if test is True:
            action()
        else:
            pl.when(test)(action)

    def both(left, right):
        return right if left is True else left if right is True else left & right

    def slot_of(dy, dz, c_):
        return ((z + dz) * 2 + (y + dy) % 2) * 2 + c_

    def held(array, owner, span):
        return up.at[span, :] if array == UP else (mix if array == MIX else out).at[owner, span, :]

    def piece(index, owner, slot):
        array, start, count = plan[index][:3]
        return held(array, owner, band(array, slot, start, count))

    def whole(array, owner, slot):
        return held(array, owner, band(array, slot, 0, high[array]))

    def inside(dz):
        return True if dz == 0 else (z + dz < lines) if dz > 0 else (z + dz >= 0)

    def sem_of(index, dx, slot):
        kind = pieces + index - lead[plan[index][0]] if dx else index
        return recv_sem.at[slot // 2 * (kinds + 4) + kind]

    def whole_sem(array, dx, slot):
        return recv_sem.at[slot // 2 * (kinds + 4) + kinds + (3 if dx else array)]

    turned = z // (lines // 2)
    folded = z + turned * (lines - 1 - 2 * z)

    def plane_of(reach):
        near_plane = folded if reach == 0 else 1 - folded if reach == 1 else reach
        return near_plane + turned * (lines - 1 - 2 * near_plane)

    def columns(index, count):
        return pl.ds(pl.multiple_of(index * count, count), count)

    def fold(product):
        sums = product[:, :128]
        for start in range(128, product.shape[1], 128):
            sums = sums + product[:, start:start + 128]
        return sums

    step = width

    def blocks(action, size=step):
        def run(index, carry):
            action(index)
            return carry

        lax.fori_loop(0, features // size, run, 0, unroll=4)

    def mean_of(sums):
        return jnp.sum(sums[...], axis=1, keepdims=True) / features

    def ups():
        return up[...]

    def block_of_out(owner, slot):
        return out[owner, band(OUT, slot, 0, width), :]

    def swap(ref):
        return pltpu.make_async_remote_copy(
            src_ref=ref,
            dst_ref=ref,
            send_sem=swap_sem.at[0],
            recv_sem=swap_sem.at[1],
            device_id=across,
            device_id_type=MESH,
        )

    acc[...] = jnp.zeros_like(acc)
    squares[...] = jnp.zeros_like(squares)
    products[...] = jnp.zeros_like(products)

    def program(sec):
        lone, common = (MIX, OUT) if sec == 0 else (OUT, MIX)

        def late(index, dx):
            return plan[index][4][sec][dx]

        def routes(index, dx, dy, dz):
            gone, result = {X: dx != 0, Y: dy != 0, Z: dz != 0}, []
            for turn, dim in enumerate(plan[index][3]):
                if any(gone[later] for later in plan[index][3][turn + 1:]):
                    continue
                if dim == Z:
                    result += [(Z, 1)] * (dz <= 0) + [(Z, -1)] * (dz >= 0)
                elif dim == Y and not gone[Y]:
                    result.append((Y, 1))
                elif dim == X and not gone[X] and plan[index][0] == common:
                    result.append((X, 1))
            return result

        def push(ref, array, way, target, sem):
            pltpu.make_async_remote_copy(
                src_ref=ref,
                dst_ref=ref,
                send_sem=send_sem.at[array * 4 + way],
                recv_sem=sem,
                device_id=target,
                device_id_type=MESH,
            ).start()

        def send_all(index, dx, dy, dz):
            slot, array = slot_of(dy, dz, core), plan[index][0]
            here = piece(index, (sec + dx) % 2, slot)
            for dim, sign in routes(index, dx, dy, dz):
                target = {Y: beside, X: across}.get(dim, above if sign > 0 else below)
                test = True if dim != Z else z + 1 < lines if sign > 0 else z > 0
                sem = sem_of(index, 1 if dim == X else dx, slot)
                when(test, functools.partial(push, here, array, dim, target, sem))

        def arrived(index, dx, slot):
            ref = piece(index, (sec + dx) % 2, slot)
            pltpu.make_async_copy(ref, ref, sem_of(index, dx, slot)).wait()

        def partners_arrived(array, dx, plane):
            for y_ in (0, 1):
                slot = (plane * 2 + y_) * 2 + 1 - core
                ref = whole(array, (sec + dx) % 2, slot)
                pltpu.make_async_copy(ref, ref, whole_sem(array, dx, slot)).wait()

        events = []
        for dx in (0, 1):
            for dy in (0, 1):
                for dz in range(1 - lines, lines):
                    for index in range(pieces):
                        if not dx or plan[index][0] == lone:
                            key = dx + dy + abs(dz) + late(index, dx)
                            events.append((key, index, dx, abs(dz), dy, dz))
        events.sort()
        closing = {(plan[index][0], dx, dy, dz): number for number, (_, index, dx, _, dy, dz) in enumerate(events)}

        def relay(number, index, dx, dy, dz):
            array, slot = plan[index][0], slot_of(dy, dz, core)

            def action():
                if dx or dy or dz:
                    arrived(index, dx, slot)
                send_all(index, dx, dy, dz)
                if closing[array, dx, dy, dz] == number:
                    push(whole(array, (sec + dx) % 2, slot), array, 3, partner, whole_sem(array, dx, slot))

            when(inside(dz), action)

        def sent_rows(array, way, z_):
            rows_ = 0
            for _, index, dx, _, dy, dz in events:
                if plan[index][0] == array and 0 <= z_ + dz < lines:
                    for dim, sign in routes(index, dx, dy, dz):
                        if dim == way and (dim != Z or 0 <= z_ + sign < lines):
                            rows_ += plan[index][2]
            if way == 3:
                rows_ = high[array] * chips * (2 if array == lone else 1)
            return rows_

        def drain_sends():
            for array in high:
                for way in (X, Y, Z, 3):
                    for fold_ in range(lines // 2):
                        rows_ = sent_rows(array, way, fold_)
                        if not rows_ or (way != Z and fold_):
                            continue

                        def wait(rows_=rows_, array=array, way=way):
                            ref = held(array, 0, pl.ds(0, rows_))
                            pltpu.make_async_copy(ref, ref, send_sem.at[array * 4 + way]).wait()

                        when(folded == fold_ if way == Z else True, wait)

        def ready(array, dx, reach):
            return max(dx + 1 + reach + late(index, dx) for index in range(pieces) if plan[index][0] == array)

        def prepare():
            for copy in inputs_staged:
                copy.wait()
            if sec:
                return

            def square(index):
                entries = tok[:, columns(index, step)].astype(f32)
                squares[...] += fold(entries * entries)

            blocks(square)
            inverse = lax.rsqrt(mean_of(squares) + epsilon)

            def scale(index):
                span = columns(index, step)
                normed[:, span] = (tok[:, span].astype(f32) * inverse).astype(bf16)

            blocks(scale)
            scales[...] = jnp.broadcast_to(inverse, scales.shape)
            squares[...] = jnp.zeros_like(squares)

        def part_of(plane, part):
            return pl.ds(pl.multiple_of(plane * sheet + part * block, block), block)

        def lone_plane(reach):
            plane = plane_of(reach)
            partners_arrived(lone, 0, plane)
            if sec == 0:
                span = columns(plane, sheet)
                acc[...] += widen_dot(normed[:, span], mix[0, span, :])
                return
            sums = acc[:, :width]
            for part in range(4):
                sums = sums + widen_dot(cot[:, part_of(plane, part)], block_of_out(1, plane * 4 + part), ((1,), (1,)))
            acc[:, :width] = sums

        def emit():
            for plane in range(lines):
                partners_arrived(UP, 0, plane)
            if sec == 0:
                low[...] = acc[:, width:].astype(bf16)
                vals[...] = (acc[:, :width] + widen_dot(low[...], ups(), ((1,), (1,)))).astype(bf16)
                swap(vals).start()
            else:
                cats[:, :width] = acc[:, :width].astype(bf16)
                cats[:, width:] = widen_dot(cats[:, :width], ups()).astype(bf16)
                swap(cats).start()

        def widen(reach):
            plane = plane_of(reach)
            partners_arrived(OUT, sec, plane)
            for part in range(4):
                span = part_of(plane, part)
                added = widen_dot(vals[...], block_of_out(0, plane * 4 + part))
                entries = (tok[:, span].astype(f32) + added).astype(bf16)
                states[:, span] = entries
                back = entries.astype(f32)
                squares[...] += fold(back * back)
                if sec:
                    products[...] += fold(back * wide[:, span])

        def open_up(layer, joint, span, inputs):
            entries = widen_dot(joint[...], mix[layer, span, :], ((1,), (1,)))
            wide[:, span] = entries
            if inputs is not None:
                products[...] += fold(entries * inputs[:, span].astype(f32))

        def open_plane(reach):
            plane = plane_of(reach)
            partners_arrived(MIX, 1 - sec, plane)
            for part in range(2):
                span = pl.ds(pl.multiple_of(plane * sheet + part * step, step), step)
                open_up(1, cats, span, states if sec == 0 else None)

        def scoped(name, action, *args):
            with jax.named_scope(name):
                action(*args)

        timeline = [(key, 0, number, "relay%d" % int(key), functools.partial(relay, number, *event[:2], *event[3:]))
                    for number, (key, *event) in enumerate(events)]
        emitted = ready(lone, 0, lines - 1) + 0.02
        timeline.append((0.01, 1, 0, "prepare", prepare))
        timeline.append((emitted, 2, 0, "emit", emit))
        for reach in range(lines):
            timeline.append((ready(lone, 0, reach), 1, reach, "lone", functools.partial(lone_plane, reach)))
            early, behind = (widen, open_plane) if sec == 0 else (open_plane, widen)
            key = max(ready(common, 0, reach), emitted)
            timeline.append((key, 3, reach, early.__name__, functools.partial(early, reach)))
            timeline.append((1000, 2, reach, behind.__name__, functools.partial(behind, reach)))
        timeline.append((1000, 1, 0, "swapped", swap(vals).wait_recv if sec else swap(cats).wait_recv))
        timeline.sort(key=lambda item: item[:3])
        for _, _, _, name, action in timeline:
            scoped(name, action)

        def gradients(joint):
            turned_low = joint[:, width:].T
            for index in range(fsdp):
                product = widen_dot(turned_low, normed[:, index * block:(index + 1) * block]).astype(bf16)
                for start in range(0, block, rank):
                    parts[index % 2, index // 4, index // 2 % 2, start:start + rank, :] = product[:, start:start + rank]
            ends = widen_dot(joint[:, :width], low[...], ((0,), (0,))).astype(bf16)
            for index in range(fsdp):
                owned = ends[index * share_up:(index + 1) * share_up]
                parts[index % 2, index // 4, index // 2 % 2, block:, :] = owned

        handed, sided, passed = [], [], []
        half = lines // 2

        def settle():
            for turn in (0, 1):
                span = pl.ds((turned + 1 + turn) % 2 * half, half)
                copy = pltpu.make_async_remote_copy(
                    src_ref=parts.at[1 - core, span],
                    dst_ref=near.at[span],
                    send_sem=near_sem.at[2 + turn],
                    recv_sem=near_sem.at[turn],
                    device_id=partner,
                    device_id_type=MESH,
                )
                copy.start()
                handed.append(copy)
            for turn in range(lines):
                if turn % half == 0:
                    handed[turn // half].wait_recv()
                plane = plane_of(lines - 1 - turn)
                mine[plane] = (parts[core, plane, 1 - y].astype(f32) + near[plane, 1 - y].astype(f32)).astype(bf16)
                copy = pltpu.make_async_remote_copy(
                    src_ref=mine.at[plane],
                    dst_ref=beside_sums.at[plane],
                    send_sem=side_sem.at[lines + turn],
                    recv_sem=side_sem.at[turn],
                    device_id=beside,
                    device_id_type=MESH,
                )
                sided.append(copy)
                if turn:
                    sided[turn - 1].start()
            sided[-1].start()

        def pass_on():
            for turn in range(lines):
                sided[turn].wait_recv()
                plane = plane_of(lines - 1 - turn)
                sums = parts[core, plane, y].astype(f32) + near[plane, y].astype(f32) + beside_sums[plane].astype(f32)
                if turn == lines - 1:
                    total[...] = sums
                    continue
                sent[turn] = sums.astype(bf16)
                copy = pltpu.make_async_remote_copy(
                    src_ref=sent.at[turn],
                    dst_ref=far.at[z],
                    send_sem=far_sem.at[lines + turn],
                    recv_sem=far_sem.at[z],
                    device_id=place(s, plane, y, core),
                    device_id_type=MESH,
                )
                copy.start()
                passed.append(copy)

        def write_flow():
            copy = pltpu.make_async_copy(flow, flow_any, local_sem.at[0])
            copy.start()
            return copy

        inverse = lax.rsqrt(mean_of(squares) + epsilon)

        def upstream_of(span, factor):
            inputs = states[:, span].astype(f32)
            entries = cot[:, span].astype(f32) + inverse * (wide[:, span] - inputs * factor)
            flow[:, span] = entries.astype(bf16)

        acc[...] = jnp.zeros_like(acc)
        factor = inverse * inverse * mean_of(products)
        if sec == 0:
            def narrow(index):
                span = columns(index, block)
                upstream_of(span, factor)
                acc[:, :width] += widen_dot(flow[:, span], block_of_out(0, index), ((1,), (1,)))

            scoped("narrow", blocks, narrow, block)
            tail[:, :width] = acc[:, :width].astype(bf16)
            tail[:, width:] = widen_dot(tail[:, :width], ups()).astype(bf16)
            scoped("grads", gradients, tail)
            scoped("settle", settle)
            products[...] = jnp.zeros_like(products)
            scoped("open0", blocks, lambda index: open_up(0, tail, columns(index, step), tok))
            scoped("pass", pass_on)
            first_inverse = scales[:, :1]
            first_factor = first_inverse * first_inverse * mean_of(products)

            def finish(index):
                span = columns(index, step)
                change = wide[:, span] - tok[:, span].astype(f32) * first_factor
                flow[:, span] = (flow[:, span].astype(f32) + first_inverse * change).astype(bf16)

            scoped("finish", blocks, finish)
            flow_copy = write_flow()
        else:
            def lower(index):
                span = columns(index, step)
                normed[:, span] = (states[:, span].astype(f32) * inverse).astype(bf16)
                acc[:, width:] += widen_dot(normed[:, span], mix[1, span, width:])

            scoped("lower", blocks, lower)
            low[...] = acc[:, width:].astype(bf16)
            scoped("grads", gradients, cats)
            scoped("settle", settle)
            scoped("upstream", blocks, lambda index: upstream_of(columns(index, step), factor))
            flow_copy = write_flow()
            scoped("pass", pass_on)

        def settled():
            for reach in range(1, lines):
                plane = plane_of(reach)
                pltpu.make_async_copy(far.at[plane], far.at[plane], far_sem.at[plane]).wait()
                total[...] += far[plane].astype(f32)

        scoped("settled", settled)
        grad_copy = pltpu.make_async_copy(total, grad_any, local_sem.at[1])
        grad_copy.start()

        def drain():
            drain_sends()
            (swap(cats) if sec else swap(vals)).wait_send()
            for copy in handed + sided + passed:
                copy.wait_send()
            flow_copy.wait()
            grad_copy.wait()

        scoped("drain", drain)

    for sec in (0, 1):
        pl.when(s == sec)(functools.partial(program, sec))


def finish_kernel(micro, order_ref, flow_ref, grad_ref, out_ref, down_ref, up_ref):
    local = flow_ref.shape[0] // micro
    for slot in range(micro):
        out_ref[slot] = flow_ref[pl.ds(pl.multiple_of(order_ref[slot] * local, local), local), :]
    split = down_ref.shape[0]
    rank = down_ref.shape[1]
    for start in range(0, split, rank):
        down_ref[start:start + rank, :] = grad_ref[start:start + rank, :].T
    up_ref[...] = grad_ref[split:]


def custom_route():
    fsdp = lax.axis_size("fsdp")
    return lax.axis_size("section") == 2 and fsdp % 8 == 0 and fsdp <= 16


def run_custom(tokens, cotangent, order, value, down, out, up):
    micro, local, features = tokens.shape
    rows = micro * local
    fsdp = lax.axis_size("fsdp")
    lines, chips = fsdp // 4, fsdp // 2
    block, width = value.shape
    rank = down.shape[1]
    share_up = up.shape[0]
    both, high = width + rank, block + share_up
    plan = plan_of(width, block, share_up)
    most = max(sum(item[0] == array for item in plan) for array in (OUT, MIX))
    outside, inside = pl.BlockSpec(memory_space=pl.ANY), pl.BlockSpec(memory_space=pltpu.VMEM)
    dma = pltpu.SemaphoreType.DMA
    vmem = pltpu.VMEM
    flow, grads = pl.pallas_call(
        functools.partial(relay_kernel, lines, plan),
        out_shape=[
            jax.ShapeDtypeStruct((rows, features), bf16),
            jax.ShapeDtypeStruct((high, rank), f32),
        ],
        in_specs=[outside] * 6,
        out_specs=[outside] * 2,
        scratch_shapes=[
            vmem((2, features, both), bf16),
            vmem((2, fsdp * width, block), bf16),
            vmem((fsdp * share_up, rank), bf16),
            vmem((rows, features), bf16),
            vmem((rows, features), bf16),
            vmem((rows, features), bf16),
            vmem((rows, features), bf16),
            vmem((rows, features), f32),
            vmem((rows, features), bf16),
            vmem((rows, both), f32),
            vmem((rows, width), bf16),
            vmem((rows, both), bf16),
            vmem((rows, both), bf16),
            vmem((rows, rank), bf16),
            vmem((rows, 128), f32),
            vmem((rows, 128), f32),
            vmem((rows, 128), f32),
            vmem((2, lines, 2, high, rank), bf16),
            vmem((lines, 2, high, rank), bf16),
            vmem((lines, high, rank), bf16),
            vmem((lines, high, rank), bf16),
            vmem((lines, high, rank), bf16),
            vmem((lines, high, rank), bf16),
            vmem((high, rank), f32),
            dma((6,)),
            dma((chips * (len(plan) + most + 4),)),
            dma((12,)),
            dma((2,)),
            dma((4,)),
            dma((lines * 2,)),
            dma((lines * 2,)),
        ],
        compiler_params=pltpu.CompilerParams(
            collective_id=0, has_side_effects=True, vmem_limit_bytes=67_000_000
        ),
    )(tokens.reshape(rows, features), cotangent.reshape(rows, features), value, down, out, up)
    return pl.pallas_call(
        functools.partial(finish_kernel, micro),
        out_shape=[
            jax.ShapeDtypeStruct((micro, local, features), bf16),
            jax.ShapeDtypeStruct((block, rank), f32),
            jax.ShapeDtypeStruct((share_up, rank), f32),
        ],
        in_specs=[pl.BlockSpec(memory_space=pltpu.SMEM), inside, inside],
        out_specs=[inside] * 3,
    )(order, flow, grads)


def gather_weights(w_value, w_out, adapter_down, adapter_up):
    sections = lax.axis_size("section")

    def whole(block):
        full = lax.all_gather(block, ("section", "fsdp"), axis=0, tiled=True)
        return full.reshape(sections, -1, block.shape[1])

    joined = jnp.concatenate([w_value[0], adapter_down[0]], axis=1)
    return whole(joined), whole(w_out[0].T), whole(adapter_up[0].T)


def body(tokens, cotangent, order, w_value, w_out, adapter_down, adapter_up):
    sections = lax.axis_size("section")
    position = lax.axis_index("section")
    micro, local, features = tokens.shape
    width = w_value.shape[2]

    if custom_route():
        out, grad_down, grad_up = run_custom(
            tokens, cotangent, order, w_value[0], adapter_down[0], w_out[0], adapter_up[0].T
        )
        return (out[None], grad_down[None], grad_up.T[None])

    joined, proj, up = gather_weights(w_value, w_out, adapter_down, adapter_up)
    current = tokens.reshape(micro * local, features)
    saved = []
    for layer in range(sections):
        widened = current.astype(jnp.float32)
        inverse = lax.rsqrt(jnp.mean(widened * widened, axis=-1, keepdims=True) + epsilon)
        normed = (widened * inverse).astype(jnp.bfloat16)
        last = layer == sections - 1
        if last:
            low = widen_dot(normed, joined[layer][:, width:]).astype(jnp.bfloat16)
        else:
            both = widen_dot(normed, joined[layer])
            low = both[:, width:].astype(jnp.bfloat16)
            values = (both[:, :width] + widen_dot(low, up[layer], ((1,), (1,)))).astype(jnp.bfloat16)
        saved.append((current, normed, low, inverse))
        if not last:
            current = (widened + widen_dot(values, proj[layer], ((1,), (1,)))).astype(jnp.bfloat16)

    upstream = cotangent.reshape(micro * local, features)
    grads, d_vals, d_lows = [], [], []
    for layer in reversed(range(sections)):
        inputs, normed, low, inverse = saved[layer]
        d_values = widen_dot(upstream, proj[layer]).astype(jnp.bfloat16)
        d_low = widen_dot(d_values, up[layer]).astype(jnp.bfloat16)
        d_normed = widen_dot(
            jnp.concatenate([d_values, d_low], axis=1), joined[layer], ((1,), (1,))
        )
        widened = inputs.astype(jnp.float32)
        project = jnp.mean(d_normed * widened, axis=-1, keepdims=True)
        upstream = (
            upstream.astype(jnp.float32)
            + inverse * (d_normed - widened * inverse * inverse * project)
        ).astype(jnp.bfloat16)
        grads.insert(0, upstream)
        d_vals.insert(0, d_values)
        d_lows.insert(0, d_low)

    def mine(items):
        chosen = items[0]
        for layer in range(1, sections):
            chosen = jnp.where(position == layer, items[layer], chosen)
        return chosen

    shares = lax.axis_size("fsdp")
    normed = mine([item[1] for item in saved])
    low = mine([item[2] for item in saved])
    part_down = widen_dot(normed, mine(d_lows), ((0,), (0,)))
    part_up = widen_dot(mine(d_vals), low, ((0,), (0,)))
    rank = low.shape[1]
    parts = jnp.concatenate(
        [part_down.reshape(shares, -1, rank), part_up.reshape(shares, -1, rank)], axis=1
    )
    share_down = features // shares
    combined = lax.psum_scatter(parts, "fsdp", scatter_dimension=0, tiled=True)[0]
    grad_down, grad_up = combined[:share_down], combined[share_down:]
    out = mine(grads).reshape(micro, local, features)[order]
    return (out[None], grad_down[None], grad_up.T[None])


def solution(mesh):
    return jax.shard_map(
        body,
        mesh=mesh,
        in_specs=(
            P(None, "fsdp", None),
            P(None, "fsdp", None),
            P(),
            P("section", "fsdp", None),
            P("section", None, "fsdp"),
            P("section", "fsdp", None),
            P("section", None, "fsdp"),
        ),
        out_specs=(
            P("section", None, "fsdp", None),
            P("section", "fsdp", None),
            P("section", None, "fsdp"),
        ),
        check_vma=False,
    )
```

time: 109 us -> 85.6 us (0.79)
  the two profiles are of different devices: /device:TPU:15 before, /device:TPU:0 now
where the time goes in v2:
time: 85.6 us; the launch traced here: 85.4 us
  Pallas kernels  84.8 us (99%)
    pallas_call x1, Pallas kernels, run_custom(): pl.pallas_call(functools.partial(relay_kernel, lines, plan), out_shape=[j...  82.1 us
    pallas_call x1, Pallas kernels, run_custom(): pl.pallas_call(functools.partial(finish_kernel, micro), out_shape=[jax.Sh...  2.72 us

profile of v2, /device:TPU:0, one launch (start us, length us, event | category | flops | bytes accessed | tf_op | source)
XLA Modules:
  0.0 85.4 jit_solution(17984164201889878079)
XLA Ops:
  0.6 82.1 %shard_map.94 = (bf16[192,4096]{1,0:T(8,128)(2,1)}, f32[288,128]{1,0:T(8,128)}) custom-call(bf16[192,4096]{1,0:T(8,128)(2,1)} %bitcast.13, bf16[192,4096]{1,0:T(8,128)(2,1)} %bitcast.14, bf16[256,512]{1,0:T(8,128)(2,1)} %bitcast.15, bf16[256,128]{1,0:T(8,128)(2,1)} %bitcast.17, bf16[512,256]{1,0:T(8,128)(2,1)} %bitcast.16, bf16[32,128]{1,0:T(8,128)(2,1)} %bitcast.18), custom_call_target="tpu_custom_call" | custom-call | tf_op jit(solution)/shard_map/pallas_call | solution.py:551
  82.7 2.7 %shard_map.95 = (bf16[6,32,4096]{2,1,0:T(8,128)(2,1)}, f32[256,128]{1,0:T(8,128)}, f32[32,128]{1,0:T(8,128)}) custom-call(s32[6]{0:T(128)} %order_ref.1, bf16[192,4096]{1,0:T(8,128)(2,1)} %get-tuple-element.8.flow_ref, f32[288,128]{1,0:T(8,128)} %get-tuple-element.9.grad_ref), custom_call_target="tpu_custom_call" | custom-call | tf_op jit(solution)/shard_map/pallas_call | solution.py:596

commit v3 on v2

--- a/solution.py
+++ b/solution.py
@@ -27,9 +27,9 @@
             start += count
         return result
 
-    none = ((0, 0), (0, 0))
+    soon = ((-1, 0), (-1, 0))
     return tuple(
-        cut(UP, up_rows, [(32, (Z, Y), none)])
+        cut(UP, up_rows, [(32, (Z, Y), soon)])
         + cut(OUT, out_rows, [
                 (7, (Z, Y, X), ((-0.25, -1.0), (-0.25, 2.0))),
                 (10, (Z, Y, X), ((0, 0.25), (0, 0.0))),
@@ -94,12 +94,19 @@
     inputs_staged = [stage(tok_any, tok, 4), stage(cot_any, cot, 5)]
 
     barrier = pltpu.get_barrier_semaphore()
-    for target in (partner, across):
+    for target in (partner, across, beside):
         pl.semaphore_signal(barrier, inc=1, device_id=target, device_id_type=MESH)
-    for step in range(1, chips):
-        target = {"section": s, "fsdp": ((chip + step) % chips) * 2 + core}
-        pl.semaphore_signal(barrier, inc=1, device_id=target, device_id_type=MESH)
-    pl.semaphore_wait(barrier, chips + 1)
+
+    @pl.when(z + 1 < lines)
+    def _():
+        pl.semaphore_signal(barrier, inc=1, device_id=above, device_id_type=MESH)
+
+    @pl.when(z > 0)
+    def _():
+        pl.semaphore_signal(barrier, inc=1, device_id=below, device_id_type=MESH)
+
+    ends = (z + 1 < lines).astype(jnp.int32) + (z > 0).astype(jnp.int32)
+    pl.semaphore_wait(barrier, 3 + ends)
     for array in (UP, OUT, MIX):
         for copy in staged[array]:
             copy.wait()
@@ -363,16 +370,20 @@
 
         timeline = [(key, 0, number, "relay%d" % int(key), functools.partial(relay, number, *event[:2], *event[3:]))
                     for number, (key, *event) in enumerate(events)]
-        emitted = ready(lone, 0, lines - 1) + 0.02
+        emitted = max(ready(lone, 0, lines - 1), ready(UP, 0, lines - 1)) + 0.02
+        swapped = (1000, 1000)[sec]
         timeline.append((0.01, 1, 0, "prepare", prepare))
         timeline.append((emitted, 2, 0, "emit", emit))
         for reach in range(lines):
-            timeline.append((ready(lone, 0, reach), 1, reach, "lone", functools.partial(lone_plane, reach)))
+            pause = 0.7 if reach < lines - 1 else 0
+            timeline.append((ready(lone, 0, reach) + pause, 1, reach, "lone", functools.partial(lone_plane, reach)))
             early, behind = (widen, open_plane) if sec == 0 else (open_plane, widen)
-            key = max(ready(common, 0, reach), emitted)
+            pause = 0.0 if reach < lines - 1 else 0
+            key = max(ready(common, 0, reach) + pause, emitted)
             timeline.append((key, 3, reach, early.__name__, functools.partial(early, reach)))
-            timeline.append((1000, 2, reach, behind.__name__, functools.partial(behind, reach)))
-        timeline.append((1000, 1, 0, "swapped", swap(vals).wait_recv if sec else swap(cats).wait_recv))
+            key = max(ready(lone, 1, reach), swapped)
+            timeline.append((key, 4, reach, behind.__name__, functools.partial(behind, reach)))
+        timeline.append((swapped, 3, 9, "swapped", swap(vals).wait_recv if sec else swap(cats).wait_recv))
         timeline.sort(key=lambda item: item[:3])
         for _, _, _, name, action in timeline:
             scoped(name, action)
@@ -457,14 +468,16 @@
         acc[...] = jnp.zeros_like(acc)
         factor = inverse * inverse * mean_of(products)
         if sec == 0:
-            def narrow(index):
-                span = columns(index, block)
-                upstream_of(span, factor)
-                acc[:, :width] += widen_dot(flow[:, span], block_of_out(0, index), ((1,), (1,)))
-
-            scoped("narrow", blocks, narrow, block)
-            tail[:, :width] = acc[:, :width].astype(bf16)
-            tail[:, width:] = widen_dot(tail[:, :width], ups()).astype(bf16)
+            def narrow():
+                sums = jnp.zeros((rows, width), f32)
+                for index in range(fsdp):
+                    span = slice(index * block, (index + 1) * block)
+                    upstream_of(span, factor)
+                    sums = sums + widen_dot(flow[:, span], out[0, index * width:(index + 1) * width, :], ((1,), (1,)))
+                tail[:, :width] = sums.astype(bf16)
+                tail[:, width:] = widen_dot(tail[:, :width], ups()).astype(bf16)
+
+            scoped("narrow", narrow)
             scoped("grads", gradients, tail)
             scoped("settle", settle)
             products[...] = jnp.zeros_like(products)

time: 85.6 us -> 82.3 us (0.961)
  Pallas kernels: 84.8 us -> 81.5 us
    pallas_call x1, Pallas kernels: 82.1 us -> 78.8 us  [run_custom(): pl.pallas_call(functools.partial(relay_kernel, lines, plan), out_shape=[j...]
where the time goes in v3:
time: 82.3 us; the launch traced here: 82.2 us
  Pallas kernels  81.5 us (99%)
    pallas_call x1, Pallas kernels, run_custom(): pl.pallas_call(functools.partial(relay_kernel, lines, plan), out_shape=[j...  78.8 us
    pallas_call x1, Pallas kernels, run_custom(): pl.pallas_call(functools.partial(finish_kernel, micro), out_shape=[jax.Sh...  2.72 us

profile of v3, /device:TPU:0, one launch (start us, length us, event | category | flops | bytes accessed | tf_op | source)
XLA Modules:
  0.0 82.2 jit_solution(2399214855945240848)
XLA Ops:
  0.6 78.8 %shard_map.94 = (bf16[192,4096]{1,0:T(8,128)(2,1)}, f32[288,128]{1,0:T(8,128)}) custom-call(bf16[192,4096]{1,0:T(8,128)(2,1)} %bitcast.13, bf16[192,4096]{1,0:T(8,128)(2,1)} %bitcast.14, bf16[256,512]{1,0:T(8,128)(2,1)} %bitcast.15, bf16[256,128]{1,0:T(8,128)(2,1)} %bitcast.17, bf16[512,256]{1,0:T(8,128)(2,1)} %bitcast.16, bf16[32,128]{1,0:T(8,128)(2,1)} %bitcast.18), custom_call_target="tpu_custom_call" | custom-call | tf_op jit(solution)/shard_map/pallas_call | solution.py:564
  79.4 2.7 %shard_map.95 = (bf16[6,32,4096]{2,1,0:T(8,128)(2,1)}, f32[256,128]{1,0:T(8,128)}, f32[32,128]{1,0:T(8,128)}) custom-call(s32[6]{0:T(128)} %order_ref.1, bf16[192,4096]{1,0:T(8,128)(2,1)} %get-tuple-element.8.flow_ref, f32[288,128]{1,0:T(8,128)} %get-tuple-element.9.grad_ref), custom_call_target="tpu_custom_call" | custom-call | tf_op jit(solution)/shard_map/pallas_call | solution.py:609

commit v4 on v3

--- a/solution.py
+++ b/solution.py
@@ -27,20 +27,19 @@
             start += count
         return result
 
-    soon = ((-1, 0), (-1, 0))
+    soon = ((-1, 0, -1), (-1, 0, -1))
     return tuple(
         cut(UP, up_rows, [(32, (Z, Y), soon)])
         + cut(OUT, out_rows, [
-                (7, (Z, Y, X), ((-0.25, -1.0), (-0.25, 2.0))),
-                (10, (Z, Y, X), ((0, 0.25), (0, 0.0))),
-                (8, (Y, Z, X), ((0.5, 0), (-0.75, 1.25))),
-                (7, (X, Z, Y), ((2, -1.5), (0.25, 1.75))),
+                (15, (Z, Y, X), ((-0.25, 0.5, 0.25), (-0.25, -0.75, -1))),
+                (9, (Y, Z, X), ((1.25, 0.25, -0.25), (-1, 2.5, -6.5))),
+                (8, (X, Z, Y), ((2.0, -0.25, -1.75), (-1.25, 1.5, -2.25))),
             ])
         + cut(MIX, mix_rows, [
-                (8, (Z, Y, X), ((-0.5, 2.5), (0.75, 1.25))),
-                (16, (Z, Y, X), ((0.25, -0.5), (-1, 0.75))),
-                (4, (X, Z, Y), ((0, 1.5), (1.5, 2.0))),
-                (4, (X, Y, Z), ((-0.25, 2), (2, -1))),
+                (10, (Z, Y, X), ((0.0, 2.5, -0.75), (0.5, 0.5, -0.25))),
+                (16, (Z, Y, X), ((0.25, -0.75, 0.25), (-2.0, -0.25, -3.0))),
+                (2, (X, Z, Y), ((0.25, 0.75, 0.25), (1.5, 1.5, 1.25))),
+                (4, (X, Y, Z), ((-0.75, 2.0, -0.75), (2, -2.0, 0.75))),
             ])
     )
 
@@ -197,6 +196,10 @@
         def late(index, dx):
             return plan[index][4][sec][dx]
 
+        def key_of(index, dx, dy, dz):
+            reach = dx + dy + abs(dz)
+            return reach + plan[index][4][sec][dx if reach else 2]
+
         def routes(index, dx, dy, dz):
             gone, result = {X: dx != 0, Y: dy != 0, Z: dz != 0}, []
             for turn, dim in enumerate(plan[index][3]):
@@ -220,10 +223,12 @@
                 device_id_type=MESH,
             ).start()
 
-        def send_all(index, dx, dy, dz):
+        def send_all(index, dx, dy, dz, dims=(X, Y, Z)):
             slot, array = slot_of(dy, dz, core), plan[index][0]
             here = piece(index, (sec + dx) % 2, slot)
             for dim, sign in routes(index, dx, dy, dz):
+                if dim not in dims:
+                    continue
                 target = {Y: beside, X: across}.get(dim, above if sign > 0 else below)
                 test = True if dim != Z else z + 1 < lines if sign > 0 else z > 0
                 sem = sem_of(index, 1 if dim == X else dx, slot)
@@ -245,8 +250,7 @@
                 for dz in range(1 - lines, lines):
                     for index in range(pieces):
                         if not dx or plan[index][0] == lone:
-                            key = dx + dy + abs(dz) + late(index, dx)
-                            events.append((key, index, dx, abs(dz), dy, dz))
+                            events.append((key_of(index, dx, dy, dz), index, dx, abs(dz), dy, dz))
         events.sort()
         closing = {(plan[index][0], dx, dy, dz): number for number, (_, index, dx, _, dy, dz) in enumerate(events)}
 
@@ -256,7 +260,9 @@
             def action():
                 if dx or dy or dz:
                     arrived(index, dx, slot)
-                send_all(index, dx, dy, dz)
+                    send_all(index, dx, dy, dz)
+                else:
+                    send_all(index, dx, dy, dz, (Y, Z))
                 if closing[array, dx, dy, dz] == number:
                     push(whole(array, (sec + dx) % 2, slot), array, 3, partner, whole_sem(array, dx, slot))
 
@@ -288,7 +294,11 @@
                         when(folded == fold_ if way == Z else True, wait)
 
         def ready(array, dx, reach):
-            return max(dx + 1 + reach + late(index, dx) for index in range(pieces) if plan[index][0] == array)
+            keys = [
+                max(dx + 1 + reach + late(index, dx), plan[index][4][sec][2 * (not dx)])
+                for index in range(pieces) if plan[index][0] == array
+            ]
+            return max(keys)
 
         def prepare():
             for copy in inputs_staged:
@@ -354,15 +364,21 @@
         def open_up(layer, joint, span, inputs):
             entries = widen_dot(joint[...], mix[layer, span, :], ((1,), (1,)))
             wide[:, span] = entries
-            if inputs is not None:
-                products[...] += fold(entries * inputs[:, span].astype(f32))
-
-        def open_plane(reach):
-            plane = plane_of(reach)
-            partners_arrived(MIX, 1 - sec, plane)
-            for part in range(2):
-                span = pl.ds(pl.multiple_of(plane * sheet + part * step, step), step)
-                open_up(1, cats, span, states if sec == 0 else None)
+            products[...] += fold(entries * inputs[:, span].astype(f32))
+
+        def open_planes(*reaches):
+            planes = [plane_of(reach) for reach in reaches]
+            for plane in planes:
+                partners_arrived(MIX, 1 - sec, plane)
+            sums = products[...]
+            for plane in planes:
+                for part in range(2):
+                    span = pl.ds(pl.multiple_of(plane * sheet + part * step, step), step)
+                    entries = widen_dot(cats[...], mix[1, span, :], ((1,), (1,)))
+                    wide[:, span] = entries
+                    if sec == 0:
+                        sums = sums + fold(entries * states[:, span].astype(f32))
+            products[...] = sums
 
         def scoped(name, action, *args):
             with jax.named_scope(name):
@@ -371,53 +387,52 @@
         timeline = [(key, 0, number, "relay%d" % int(key), functools.partial(relay, number, *event[:2], *event[3:]))
                     for number, (key, *event) in enumerate(events)]
         emitted = max(ready(lone, 0, lines - 1), ready(UP, 0, lines - 1)) + 0.02
-        swapped = (1000, 1000)[sec]
         timeline.append((0.01, 1, 0, "prepare", prepare))
         timeline.append((emitted, 2, 0, "emit", emit))
         for reach in range(lines):
-            pause = 0.7 if reach < lines - 1 else 0
-            timeline.append((ready(lone, 0, reach) + pause, 1, reach, "lone", functools.partial(lone_plane, reach)))
-            early, behind = (widen, open_plane) if sec == 0 else (open_plane, widen)
-            pause = 0.0 if reach < lines - 1 else 0
-            key = max(ready(common, 0, reach) + pause, emitted)
-            timeline.append((key, 3, reach, early.__name__, functools.partial(early, reach)))
-            key = max(ready(lone, 1, reach), swapped)
-            timeline.append((key, 4, reach, behind.__name__, functools.partial(behind, reach)))
-        timeline.append((swapped, 3, 9, "swapped", swap(vals).wait_recv if sec else swap(cats).wait_recv))
+            timeline.append((ready(lone, 0, reach), 1, reach, "lone", functools.partial(lone_plane, reach)))
+            key = max(ready(common, 0, reach), emitted)
+            if sec == 0:
+                timeline.append((key, 3, reach, "widen", functools.partial(widen, reach)))
+            else:
+                timeline.append((key, 3, reach, "open", functools.partial(open_planes, reach)))
+                timeline.append((1000, 4, reach, "widen", functools.partial(widen, reach)))
+        if sec == 0:
+            timeline.append((1000, 4, 0, "open", functools.partial(open_planes, *range(lines - 1))))
+            timeline.append((1000, 4, 1, "open", functools.partial(open_planes, lines - 1)))
+        timeline.append((1000, 3, 0, "swapped", swap(vals).wait_recv if sec else swap(cats).wait_recv))
         timeline.sort(key=lambda item: item[:3])
+        for index in range(pieces):
+            send_all(index, 0, 0, 0, (X,))
         for _, _, _, name, action in timeline:
             scoped(name, action)
 
-        def gradients(joint):
+        handed, sided, passed = [], [], []
+
+        def settle(joint):
             turned_low = joint[:, width:].T
-            for index in range(fsdp):
-                product = widen_dot(turned_low, normed[:, index * block:(index + 1) * block]).astype(bf16)
-                for start in range(0, block, rank):
-                    parts[index % 2, index // 4, index // 2 % 2, start:start + rank, :] = product[:, start:start + rank]
-            ends = widen_dot(joint[:, :width], low[...], ((0,), (0,))).astype(bf16)
-            for index in range(fsdp):
-                owned = ends[index * share_up:(index + 1) * share_up]
-                parts[index % 2, index // 4, index // 2 % 2, block:, :] = owned
-
-        handed, sided, passed = [], [], []
-        half = lines // 2
-
-        def settle():
-            for turn in (0, 1):
-                span = pl.ds((turned + 1 + turn) % 2 * half, half)
+            for turn in range(lines):
+                plane = plane_of(lines - 1 - turn)
+                ends = widen_dot(joint[:, columns(plane, share_up * 4)], low[...], ((0,), (0,))).astype(bf16)
+                for part in range(4):
+                    product = widen_dot(turned_low, normed[:, part_of(plane, part)]).astype(bf16)
+                    for start in range(0, block, rank):
+                        parts[part % 2, plane, part // 2, start:start + rank, :] = product[:, start:start + rank]
+                    parts[part % 2, plane, part // 2, block:, :] = ends[part * share_up:(part + 1) * share_up]
                 copy = pltpu.make_async_remote_copy(
-                    src_ref=parts.at[1 - core, span],
-                    dst_ref=near.at[span],
-                    send_sem=near_sem.at[2 + turn],
+                    src_ref=parts.at[1 - core, plane],
+                    dst_ref=near.at[plane],
+                    send_sem=near_sem.at[lines + turn],
                     recv_sem=near_sem.at[turn],
                     device_id=partner,
                     device_id_type=MESH,
                 )
-                copy.start()
                 handed.append(copy)
+                if turn:
+                    handed[turn - 1].start()
+            handed[-1].start()
             for turn in range(lines):
-                if turn % half == 0:
-                    handed[turn // half].wait_recv()
+                handed[turn].wait_recv()
                 plane = plane_of(lines - 1 - turn)
                 mine[plane] = (parts[core, plane, 1 - y].astype(f32) + near[plane, 1 - y].astype(f32)).astype(bf16)
                 copy = pltpu.make_async_remote_copy(
@@ -478,11 +493,9 @@
                 tail[:, width:] = widen_dot(tail[:, :width], ups()).astype(bf16)
 
             scoped("narrow", narrow)
-            scoped("grads", gradients, tail)
-            scoped("settle", settle)
+            scoped("settle", settle, tail)
             products[...] = jnp.zeros_like(products)
             scoped("open0", blocks, lambda index: open_up(0, tail, columns(index, step), tok))
-            scoped("pass", pass_on)
             first_inverse = scales[:, :1]
             first_factor = first_inverse * first_inverse * mean_of(products)
 
@@ -493,6 +506,7 @@
 
             scoped("finish", blocks, finish)
             flow_copy = write_flow()
+            scoped("pass", pass_on)
         else:
             def lower(index):
                 span = columns(index, step)
@@ -501,8 +515,7 @@
 
             scoped("lower", blocks, lower)
             low[...] = acc[:, width:].astype(bf16)
-            scoped("grads", gradients, cats)
-            scoped("settle", settle)
+            scoped("settle", settle, cats)
             scoped("upstream", blocks, lambda index: upstream_of(columns(index, step), factor))
             flow_copy = write_flow()
             scoped("pass", pass_on)
@@ -598,7 +611,7 @@
             dma((chips * (len(plan) + most + 4),)),
             dma((12,)),
             dma((2,)),
-            dma((4,)),
+            dma((lines * 2,)),
             dma((lines * 2,)),
             dma((lines * 2,)),
         ],

time: 82.3 us -> 81.7 us (level)
  no operation moved by 1% of the time
where the time goes in v4:
time: 81.7 us; the launch traced here: 81.6 us
  Pallas kernels  80.9 us (99%)
    pallas_call x1, Pallas kernels, run_custom(): pl.pallas_call(functools.partial(relay_kernel, lines, plan), out_shape=[j...  78.2 us
    pallas_call x1, Pallas kernels, run_custom(): pl.pallas_call(functools.partial(finish_kernel, micro), out_shape=[jax.Sh...  2.72 us

profile of v4, /device:TPU:0, one launch (start us, length us, event | category | flops | bytes accessed | tf_op | source)
XLA Modules:
  0.0 81.6 jit_solution(10743998225910396111)
XLA Ops:
  0.6 78.2 %shard_map.94 = (bf16[192,4096]{1,0:T(8,128)(2,1)}, f32[288,128]{1,0:T(8,128)}) custom-call(bf16[192,4096]{1,0:T(8,128)(2,1)} %bitcast.13, bf16[192,4096]{1,0:T(8,128)(2,1)} %bitcast.14, bf16[256,512]{1,0:T(8,128)(2,1)} %bitcast.15, bf16[256,128]{1,0:T(8,128)(2,1)} %bitcast.17, bf16[512,256]{1,0:T(8,128)(2,1)} %bitcast.16, bf16[32,128]{1,0:T(8,128)(2,1)} %bitcast.18), custom_call_target="tpu_custom_call" | custom-call | tf_op jit(solution)/shard_map/pallas_call | solution.py:577
  78.8 2.7 %shard_map.95 = (bf16[6,32,4096]{2,1,0:T(8,128)(2,1)}, f32[256,128]{1,0:T(8,128)}, f32[32,128]{1,0:T(8,128)}) custom-call(s32[6]{0:T(128)} %order_ref.1, bf16[192,4096]{1,0:T(8,128)(2,1)} %get-tuple-element.8.flow_ref, f32[288,128]{1,0:T(8,128)} %get-tuple-element.9.grad_ref), custom_call_target="tpu_custom_call" | custom-call | tf_op jit(solution)/shard_map/pallas_call | solution.py:622
